TPU v7x, 256 devices: a whole 4x4x8 slice. The times are simulated.
256 devices in a mesh: bank: 16 (over z, core), zero: 16 (over y, x).
Axes of the slice: x: 4, y: 4, z: 8, core: 2. Of those that a mesh axis runs over, the one named last changes fastest.
Arguments:
- master_gate: float32 [64, 2048, 1408], P('bank', 'zero'), may hold values from -0.1875 to 0.1875
- master_up: float32 [64, 2048, 1408], P('bank', 'zero'), may hold values from -0.1875 to 0.1875
- master_down: float32 [64, 1408, 2048], P('bank', None, 'zero'), may hold values from -0.21875 to 0.21875
- router_weight: float32 [2048, 64], P('zero', 'bank'), may hold values from -0.125 to 0.125
- router_gain: float32 [2048], P('zero'), may hold values from 0.25 to 1.75
Outputs:
- final_gate: bfloat16 [64, 2048, 1408], P('bank', None, 'zero')
- final_up: bfloat16 [64, 2048, 1408], P('bank', None, 'zero')
- final_down: bfloat16 [64, 1408, 2048], P('bank', 'zero')
- scale_gate: float32 [64, 1408], P('bank', 'zero')
- scale_up: float32 [64, 1408], P('bank', 'zero')
- scale_down: float32 [64, 1408], P('bank', 'zero')
- serve_router: bfloat16 [2048, 64], replicated
All inputs are finite; a program needn't handle non-finite values. Where the computation divides by a largest or mean magnitude, that divisor is 1e-20 or more.
Results may differ from a plain program's by a relative error of at most 0.0013.
Values may be sent and summed in bfloat16 or wider, within the bound.
A program may use at most 64 MiB of HBM per device.

v0:
```python
import jax
import jax.numpy as jnp
from jax import lax
from jax.sharding import PartitionSpec as P

D_MODEL = 2048


def copy_for_each(x, axis):
    count = lax.axis_size(axis)
    return lax.all_to_all(jnp.broadcast_to(x[None], (count, *x.shape)), axis, 0, 0, tiled=True)


def taken_together(x, axis):
    return copy_for_each(x, axis).sum(axis=0)


def in_one(arrays, axis):
    vector, at, finished = (jnp.concatenate([a.reshape(-1) for a in arrays]), 0, [])
    total = taken_together(vector, axis)
    for a in arrays:
        finished.append(total[at : at + a.size].reshape(a.shape))
        at += a.size
    return tuple(finished)


def side_by_side(arrays, axis, split_dim, concat_dim, along):
    both = jnp.concatenate(arrays, axis=along)
    whole, at, finished = (
        lax.all_to_all(both, axis, split_axis=split_dim, concat_axis=concat_dim, tiled=True),
        0,
        [],
    )
    for a in arrays:
        finished.append(lax.slice_in_dim(whole, at, at + a.shape[along], axis=along))
        at += a.shape[along]
    return tuple(finished)


def laid_out(pieces, dim):
    shape = list(pieces.shape[1:])
    shape[dim] *= pieces.shape[0]
    return jnp.moveaxis(pieces, 0, dim).reshape(shape)


def gather_directly(x, axis, dim):
    pieces = copy_for_each(x, axis)
    return laid_out(pieces, dim)


def local(master_gate, master_up, master_down, router_weight, router_gain):
    total_gate, total_up, total_down = in_one(
        (
            jnp.sum(jnp.abs(master_gate), axis=1),
            jnp.sum(jnp.abs(master_up), axis=1),
            jnp.sum(jnp.abs(master_down), axis=2),
        ),
        "zero",
    )
    scale_gate = total_gate / D_MODEL
    scale_up = total_up / D_MODEL
    scale_down = total_down / D_MODEL
    narrow_gate, narrow_up, narrow_down = (
        (master_gate / jnp.expand_dims(scale_gate, 1)).astype(jnp.bfloat16),
        (master_up / jnp.expand_dims(scale_up, 1)).astype(jnp.bfloat16),
        (master_down / jnp.expand_dims(scale_down, 2)).astype(jnp.bfloat16),
    )
    final_gate, final_up = side_by_side((narrow_gate, narrow_up), "zero", 2, 1, 0)
    final_down = lax.all_to_all(narrow_down, "zero", split_axis=1, concat_axis=2, tiled=True)
    scale_gate = lax.dynamic_slice_in_dim(
        scale_gate, lax.axis_index("zero") * final_gate.shape[2], final_gate.shape[2], axis=1
    )
    scale_up = lax.dynamic_slice_in_dim(
        scale_up, lax.axis_index("zero") * final_up.shape[2], final_up.shape[2], axis=1
    )
    scale_down = lax.dynamic_slice_in_dim(
        scale_down, lax.axis_index("zero") * final_down.shape[1], final_down.shape[1], axis=1
    )
    part_router = (router_weight * router_gain[:, None]).astype(jnp.bfloat16)
    row_router = gather_directly(part_router, "zero", 0)
    serve_router = lax.all_gather(row_router, "bank", axis=1, tiled=True)
    return (final_gate, final_up, final_down, scale_gate, scale_up, scale_down, serve_router)


def solution(mesh):
    placed = (
        P("bank", "zero", None),
        P("bank", "zero", None),
        P("bank", None, "zero"),
        P("zero", "bank"),
        P("zero"),
    )
    return jax.shard_map(
        local,
        mesh=mesh,
        in_specs=placed,
        out_specs=(
            P("bank", None, "zero"),
            P("bank", None, "zero"),
            P("bank", "zero", None),
            P("bank", "zero"),
            P("bank", "zero"),
            P("bank", "zero"),
            P(),
        ),
        check_vma=False,
    )
```

profile of v0, /device:TPU:224, one launch (start us, length us, event | category | flops | bytes accessed | tf_op | source)
XLA Modules:
  0.0 125.6 jit_solution(8950060846199024515)
XLA Ops:
  0.6 0.0 copy-start.1
  0.6 2.2 %abs_reduce_fusion.2 = f32[4,1408]{1,0:T(4,128)S(1)} fusion(f32[4,128,1408]{2,1,0:T(8,128)} %param.5), kind=kLoop, calls=%fused_computation.4 | loop fusion | flops 1436160 | bytes 2906112 | tf_op jit(solution)/shard_map/reduce_sum | solution.py:54
  2.9 0.4 copy-done.1
  3.3 0.2 abs_reduce_fusion.1
  3.6 0.0 copy-start
  3.6 2.8 %abs_reduce_fusion = f32[4,1408]{1,0:T(4,128)S(1)} fusion(f32[4,1408,128]{2,1,0:T(8,128)} %param.7), kind=kLoop, calls=%fused_computation.2 | loop fusion | flops 1436160 | bytes 2906112 | tf_op jit(solution)/shard_map/reduce_sum | solution.py:56
  6.4 1.5 %broadcast_in_dim.4 = f32[16,1,16896]{2,1,0:T(1,128)} broadcast(f32[16896]{0:T(1024)S(1)} %pad_maximum_fusion.1), dimensions={2} | broadcast | bytes 1148928 | tf_op jit(solution)/shard_map/broadcast_in_dim | solution.py:11
  8.0 7.1 %all-to-all-start = ((f32[16,1,16896]{2,1,0:T(1,128)}), f32[16,1,16896]{2,1,0:T(1,128)}, u32[]{:S(2)}, u32[]{:S(2)}) async-start(f32[16,1,16896]{2,1,0:T(1,128)} %broadcast_in_dim.4), calls=%async_computation | async-start | bytes 2162688 | tf_op jit(solution)/shard_map/all_to_all | solution.py:11
  15.1 0.0 copy-done
  15.1 2.9 %copy.44 = f32[4,128,1408]{1,0,2:T(4,128)} copy(f32[4,128,1408]{2,1,0:T(8,128)S(1)} %copy-done) | data formatting | bytes 5767168 | tf_op args[0]
  17.9 0.0 copy-start.4
  17.9 0.0 copy-start.5
  17.9 0.0 copy-start.2
  17.9 4.6 %copy.46 = f32[4,128,1408]{1,0,2:T(4,128)} copy(f32[4,128,1408]{2,1,0:T(8,128)} %param.6) | data formatting | bytes 5767168 | tf_op args[1]
  22.6 0.0 copy-done.4
  22.6 0.0 copy-done.5
  22.6 10.6 %all-to-all-done = f32[16,1,16896]{2,1,0:T(1,128)} async-done(((f32[16,1,16896]{2,1,0:T(1,128)}), f32[16,1,16896]{2,1,0:T(1,128)}, u32[]{:S(2)}, u32[]{:S(2)}) %all-to-all-start) | async-done | bytes 1081376 | tf_op jit(solution)/shard_map/all_to_all | solution.py:11
  33.2 0.6 broadcast_in_dim.5
  33.8 3.5 %all-to-all-start.3 = ((bf16[16,128,4]{1,2,0:T(4,128)(2,1)}), bf16[16,128,4]{1,2,0:T(4,128)(2,1)S(1)}, u32[]{:S(2)}, u32[]{:S(2)}) async-start(bf16[16,128,4]{1,2,0:T(4,128)(2,1)} %broadcast_in_dim.5), calls=%async_computation.3 | async-start | bytes 32768 | tf_op jit(solution)/shard_map/all_to_all | solution.py:11
  37.3 1.9 %reduce_sum.39 = f32[16896]{0:T(1024)S(1)} reduce(f32[16,1,16896]{2,1,0:T(1,128)} %all-to-all-done, f32[]{:T(128)} %constant.6.clone.1), dimensions={0,1}, to_apply=%region_3.0 | reduce | flops 253440 | bytes 1148932 | tf_op jit(solution)/shard_map/reduce_sum | solution.py:15
  39.2 1.2 copy.50
  40.4 0.0 copy-done.2
  40.4 7.7 %fusion = bf16[4,1408,128]{2,0,1:T(4,128)(2,1)} fusion(f32[4,1408,128]{2,1,0:T(8,128)S(1)} %copy-done.2, f32[4,1408]{0,1:T(8,128)} %copy.50), kind=kLoop, calls=%fused_computation.5 | loop fusion | flops 1441792 | bytes 4347904 | tf_op jit(solution)/shard_map/convert_element_type | solution.py:66
  48.1 0.0 copy-start.3
  48.1 1.2 copy.43
  49.3 1.2 copy.45
  50.5 0.0 all-to-all-done.3
  50.5 7.2 %all-to-all-start.2 = ((bf16[4,1408,128]{2,0,1:T(4,128)(2,1)}), bf16[4,1408,128]{2,0,1:T(4,128)(2,1)}, u32[]{:S(2)}, u32[]{:S(2)}) async-start(bf16[4,1408,128]{2,0,1:T(4,128)(2,1)} %fusion), calls=%async_computation.2 | async-start | bytes 2883584 | tf_op jit(solution)/shard_map/all_to_all | solution.py:69
  57.7 0.0 copy-done.3
  57.7 6.6 %divide_convert_fusion = (bf16[4,128,1408]{1,0,2:T(4,128)(2,1)S(1)}, bf16[4,128,1408]{1,0,2:T(4,128)(2,1)S(1)}) fusion(f32[4,128,1408]{1,0,2:T(4,128)} %copy.46, f32[4,1408]{0,1:T(8,128)} %copy.45, f32[4,128,1408]{1,0,2:T(4,128)S(1)} %copy-done.3, f32[4,1408]{0,1:T(8,128)} %copy.43), kind=kLoop, calls=%fused_computation.6 | loop fusion | flops 2883584 | bytes 8695808 | tf_op jit(solution)/shard_map/convert_element_type | solution.py:65
  64.2 2.6 %pad_maximum_fusion = bf16[8,128,1408]{1,0,2:T(8,128)(2,1)} fusion(bf16[4,128,1408]{1,0,2:T(4,128)(2,1)S(1)} %get-tuple-element.12, bf16[4,128,1408]{1,0,2:T(4,128)(2,1)S(1)} %get-tuple-element.13), kind=kLoop, calls=%fused_computation | loop fusion | flops 5767168 | bytes 5767168 | tf_op jit(solution)/shard_map/concatenate | solution.py:28
  66.9 12.0 %all-to-all-done.2 = bf16[4,1408,128]{2,0,1:T(4,128)(2,1)} async-done(((bf16[4,1408,128]{2,0,1:T(4,128)(2,1)}), bf16[4,1408,128]{2,0,1:T(4,128)(2,1)}, u32[]{:S(2)}, u32[]{:S(2)}) %all-to-all-start.2) | async-done | bytes 1441824 | tf_op jit(solution)/shard_map/all_to_all | solution.py:69
  78.8 3.7 %all-to-all-start.1 = ((bf16[8,128,1408]{1,0,2:T(8,128)(2,1)}), bf16[8,128,1408]{1,0,2:T(8,128)(2,1)S(1)}, u32[]{:S(2)}, u32[]{:S(2)}) async-start(bf16[8,128,1408]{1,0,2:T(8,128)(2,1)} %pad_maximum_fusion), calls=%async_computation.1 | async-start | bytes 5767168 | tf_op jit(solution)/shard_map/all_to_all | solution.py:30
  82.6 14.6 %all-gather = bf16[16,4,2048]{2,1,0:T(4,128)(2,1)S(1)} all-gather(bf16[1,4,2048]{2,1,0:T(4,128)(2,1)S(1)} %bitcast.28), channel_id=1, replica_groups=mesh['bank'=16,'zero'=16] {'bank'}, dimensions={0}, use_global_device_ids=true | all-gather | bytes 278528 | tf_op jit(solution)/shard_map/all_gather | solution.py:81
  97.2 0.8 reshape.77
  98.0 0.6 constant_dynamic-slice_fusion.2
  98.6 0.7 constant_dynamic-slice_fusion
  99.3 3.0 %copy.52 = bf16[4,88,16,128]{3,2,1,0:T(8,128)(2,1)} copy(bf16[4,88,16,128]{3,0,1,2:T(4,128)(2,1)} %bitcast.4) | data formatting | bytes 2883584 | tf_op jit(solution)/shard_map/all_to_all | solution.py:69
  102.3 3.5 %all_to_all.38 = bf16[4,88,2048]{2,1,0:T(8,128)(2,1)} reshape(bf16[4,88,16,128]{3,2,1,0:T(8,128)(2,1)} %copy.52) | data formatting | bytes 2883584 | tf_op jit(solution)/shard_map/all_to_all | solution.py:69
  105.8 16.3 %all-to-all-done.1 = bf16[8,128,1408]{1,0,2:T(8,128)(2,1)S(1)} async-done(((bf16[8,128,1408]{1,0,2:T(8,128)(2,1)}), bf16[8,128,1408]{1,0,2:T(8,128)(2,1)S(1)}, u32[]{:S(2)}, u32[]{:S(2)}) %all-to-all-start.1) | async-done | bytes 2883616 | tf_op jit(solution)/shard_map/all_to_all | solution.py:30
  122.0 0.4 copy.47
  122.4 0.2 slice_bitcast_fusion
  122.6 1.5 %copy.64 = bf16[4,16,11,8,128]{4,3,1,2,0:T(8,128)(2,1)} copy(bf16[4,16,11,8,128]{4,3,2,1,0:T(8,128)(2,1)S(1)} %get-tuple-element.7) | data formatting | bytes 2883584 | tf_op jit(solution)/shard_map/slice | solution.py:35
  124.1 1.5 %copy.65 = bf16[4,16,11,8,128]{4,3,1,2,0:T(8,128)(2,1)} copy(bf16[4,16,11,8,128]{4,3,2,1,0:T(8,128)(2,1)S(1)} %get-tuple-element.8) | data formatting | bytes 2883584 | tf_op jit(solution)/shard_map/slice | solution.py:35
  (9 shorter events, 0.1 us)
Async XLA Ops:
  0.6 2.7 %copy-start.1 = (f32[4,128,1408]{2,1,0:T(8,128)S(1)}, f32[4,128,1408]{2,1,0:T(8,128)}, u32[]{:S(2)}) copy-start(f32[4,128,1408]{2,1,0:T(8,128)} %param.6) | copy-start | bytes 8650756
  3.6 11.5 %copy-start = (f32[4,128,1408]{2,1,0:T(8,128)S(1)}, f32[4,128,1408]{2,1,0:T(8,128)}, u32[]{:S(2)}) copy-start(f32[4,128,1408]{2,1,0:T(8,128)} %param.5) | copy-start | bytes 8650756
  8.0 25.2 %all-to-all-start = ((f32[16,1,16896]{2,1,0:T(1,128)}), f32[16,1,16896]{2,1,0:T(1,128)}, u32[]{:S(2)}, u32[]{:S(2)}) async-start(f32[16,1,16896]{2,1,0:T(1,128)} %broadcast_in_dim.4), calls=%async_computation | async-start | bytes 2162688 | tf_op jit(solution)/shard_map/all_to_all | solution.py:11
  17.9 4.7 %copy-start.4 = (f32[128,4]{0,1:T(4,128)S(1)}, f32[128,4]{0,1:T(4,128)}, u32[]{:S(2)}) copy-start(f32[128,4]{0,1:T(4,128)} %param.8) | copy-start | bytes 6148
  17.9 4.7 %copy-start.5 = (f32[128]{0:T(128)S(1)}, f32[128]{0:T(128)}, u32[]{:S(2)}) copy-start(f32[128]{0:T(128)} %param.9) | copy-start | bytes 1540
  17.9 22.5 %copy-start.2 = (f32[4,1408,128]{2,1,0:T(8,128)S(1)}, f32[4,1408,128]{2,1,0:T(8,128)}, u32[]{:S(2)}) copy-start(f32[4,1408,128]{2,1,0:T(8,128)} %param.7) | copy-start | bytes 8650756
  33.8 16.7 %all-to-all-start.3 = ((bf16[16,128,4]{1,2,0:T(4,128)(2,1)}), bf16[16,128,4]{1,2,0:T(4,128)(2,1)S(1)}, u32[]{:S(2)}, u32[]{:S(2)}) async-start(bf16[16,128,4]{1,2,0:T(4,128)(2,1)} %broadcast_in_dim.5), calls=%async_computation.3 | async-start | bytes 32768 | tf_op jit(solution)/shard_map/all_to_all | solution.py:11
  48.1 9.6 %copy-start.3 = (f32[4,128,1408]{1,0,2:T(4,128)S(1)}, f32[4,128,1408]{1,0,2:T(4,128)}, u32[]{:S(2)}) copy-start(f32[4,128,1408]{1,0,2:T(4,128)} %copy.44) | copy-start | bytes 8650756
  50.5 28.4 %all-to-all-start.2 = ((bf16[4,1408,128]{2,0,1:T(4,128)(2,1)}), bf16[4,1408,128]{2,0,1:T(4,128)(2,1)}, u32[]{:S(2)}, u32[]{:S(2)}) async-start(bf16[4,1408,128]{2,0,1:T(4,128)(2,1)} %fusion), calls=%async_computation.2 | async-start | bytes 2883584 | tf_op jit(solution)/shard_map/all_to_all | solution.py:69
  78.8 43.2 %all-to-all-start.1 = ((bf16[8,128,1408]{1,0,2:T(8,128)(2,1)}), bf16[8,128,1408]{1,0,2:T(8,128)(2,1)S(1)}, u32[]{:S(2)}, u32[]{:S(2)}) async-start(bf16[8,128,1408]{1,0,2:T(8,128)(2,1)} %pad_maximum_fusion), calls=%async_computation.1 | async-start | bytes 5767168 | tf_op jit(solution)/shard_map/all_to_all | solution.py:30
where the time goes:
time: 126 us
  waiting for transfers between devices  38.8 us (31%)
  local copies, waits for them, and re-layouts  25.8 us (20%)
  other arithmetic  24.1 us (19%)
  starting transfers between devices  21.5 us (17%)
  blocking collectives  14.6 us (12%)
    all_to_all x1, waiting for transfers between devices, side_by_side(): lax.all_to_all(both, axis, split_axis=split_dim, concat_axis=concat_dim,...  16.3 us
    all_gather x1, blocking collectives, local(): serve_router = lax.all_gather(row_router, 'bank', axis=1, tiled=True)  14.6 us
    all_to_all x1, waiting for transfers between devices, local(): lax.all_to_all(narrow_down, 'zero', split_axis=1, concat_axis=2, tiled=True)  12 us
    all_to_all x2, waiting for transfers between devices, copy_for_each(): lax.all_to_all(jnp.broadcast_to(x[None], (count, *x.shape)), axis, 0, 0,...  10.6 us
    all_to_all x2, starting transfers between devices, copy_for_each(): lax.all_to_all(jnp.broadcast_to(x[None], (count, *x.shape)), axis, 0, 0,...  10.6 us
    unnamed x16, local copies, waits for them, and re-layouts  8.94 us
    convert_element_type x1, other arithmetic, local(): (master_down / jnp.expand_dims(scale_down, 2)).astype(jnp.bfloat16)  7.73 us
    all_to_all x1, starting transfers between devices, local(): lax.all_to_all(narrow_down, 'zero', split_axis=1, concat_axis=2, tiled=True)  7.2 us
  transfers between devices with their start and end apart: 4, of which 3 were waited for; matrix products, arithmetic and copies ran while one was open for 28% of the time, Pallas kernels for 0%

commit v1 on v0

--- a/solution.py
+++ b/solution.py
@@ -78,7 +78,9 @@
     )
     part_router = (router_weight * router_gain[:, None]).astype(jnp.bfloat16)
     row_router = gather_directly(part_router, "zero", 0)
-    serve_router = lax.all_gather(row_router, "bank", axis=1, tiled=True)
+    serve_router = jnp.concatenate(
+        lax.all_to_all(jnp.stack([row_router] * lax.axis_size("bank")), "bank", 0, 0), axis=1
+    )
     return (final_gate, final_up, final_down, scale_gate, scale_up, scale_down, serve_router)
 
 

time: 126 us -> 145 us (1.15)
  the two profiles are of different devices: /device:TPU:224 before, /device:TPU:1 now
where the time goes in v1:
time: 145 us; the launch traced here: 144 us
  waiting for transfers between devices  59.3 us (41%)
  starting transfers between devices  33 us (23%)
  local copies, waits for them, and re-layouts  26 us (18%)
  other arithmetic  24.8 us (17%)
    all_to_all x1, waiting for transfers between devices, side_by_side(): lax.all_to_all(both, axis, split_axis=split_dim, concat_axis=concat_dim,...  34.2 us
    all_to_all x1, waiting for transfers between devices, local(): lax.all_to_all(narrow_down, 'zero', split_axis=1, concat_axis=2, tiled=True)  15.3 us
    all_to_all x2, starting transfers between devices, copy_for_each(): lax.all_to_all(jnp.broadcast_to(x[None], (count, *x.shape)), axis, 0, 0,...  13 us
    all_to_all x1, starting transfers between devices, local(): lax.all_to_all(jnp.stack([row_router] * lax.axis_size('bank')), 'bank', 0...  11.5 us
    all_to_all x2, waiting for transfers between devices, copy_for_each(): lax.all_to_all(jnp.broadcast_to(x[None], (count, *x.shape)), axis, 0, 0,...  9.77 us
    convert_element_type x1, other arithmetic, local(): (master_down / jnp.expand_dims(scale_down, 2)).astype(jnp.bfloat16)  7.73 us
    unnamed x11, local copies, waits for them, and re-layouts  7.58 us
    convert_element_type x1, other arithmetic, local(): (master_up / jnp.expand_dims(scale_up, 1)).astype(jnp.bfloat16)  6.56 us
  transfers between devices with their start and end apart: 5, of which 4 were waited for; matrix products, arithmetic and copies ran while one was open for 28% of the time, Pallas kernels for 0%

profile of v1, /device:TPU:1, one launch (start us, length us, event | category | flops | bytes accessed | tf_op | source)
XLA Modules:
  0.0 143.9 jit_solution(17413675191629362174)
XLA Ops:
  0.6 0.0 copy-start.1
  0.6 0.8 multiply_convert_fusion
  1.5 0.6 broadcast_in_dim.5
  2.1 7.6 %all-to-all-start.3 = ((bf16[16,128,4]{1,2,0:T(4,128)(2,1)}), bf16[16,128,4]{1,2,0:T(4,128)(2,1)S(1)}, u32[]{:S(2)}, u32[]{:S(2)}) async-start(bf16[16,128,4]{1,2,0:T(4,128)(2,1)} %broadcast_in_dim.5), calls=%async_computation.3 | async-start | bytes 32768 | tf_op jit(solution)/shard_map/all_to_all | solution.py:11
  9.7 2.1 %abs_reduce_fusion.2 = f32[4,1408]{1,0:T(4,128)S(1)} fusion(f32[4,128,1408]{2,1,0:T(8,128)} %param.5), kind=kLoop, calls=%fused_computation.4 | loop fusion | flops 1436160 | bytes 2906112 | tf_op jit(solution)/shard_map/reduce_sum | solution.py:54
  11.8 0.0 copy-done.1
  11.8 0.2 abs_reduce_fusion.1
  12.0 0.0 copy-start
  12.1 2.8 %abs_reduce_fusion = f32[4,1408]{1,0:T(4,128)S(1)} fusion(f32[4,1408,128]{2,1,0:T(8,128)} %param.7), kind=kLoop, calls=%fused_computation.2 | loop fusion | flops 1436160 | bytes 2906112 | tf_op jit(solution)/shard_map/reduce_sum | solution.py:56
  14.9 1.2 all-to-all-done.3
  16.1 1.5 %broadcast_in_dim.4 = f32[16,1,16896]{2,1,0:T(1,128)} broadcast(f32[16896]{0:T(1024)S(1)} %pad_maximum_fusion.1), dimensions={2} | broadcast | bytes 1148928 | tf_op jit(solution)/shard_map/broadcast_in_dim | solution.py:11
  17.7 5.5 %all-to-all-start = ((f32[16,1,16896]{2,1,0:T(1,128)}), f32[16,1,16896]{2,1,0:T(1,128)}, u32[]{:S(2)}, u32[]{:S(2)}) async-start(f32[16,1,16896]{2,1,0:T(1,128)} %broadcast_in_dim.4), calls=%async_computation | async-start | bytes 2162688 | tf_op jit(solution)/shard_map/all_to_all | solution.py:11
  23.1 0.0 copy-done
  23.1 2.9 %copy.44 = f32[4,128,1408]{1,0,2:T(4,128)} copy(f32[4,128,1408]{2,1,0:T(8,128)S(1)} %copy-done) | data formatting | bytes 5767168 | tf_op args[0]
  26.0 4.5 %copy.46 = f32[4,128,1408]{1,0,2:T(4,128)} copy(f32[4,128,1408]{2,1,0:T(8,128)} %param.6) | data formatting | bytes 5767168 | tf_op args[1]
  30.5 0.0 copy-start.2
  30.5 8.5 %all-to-all-done = f32[16,1,16896]{2,1,0:T(1,128)} async-done(((f32[16,1,16896]{2,1,0:T(1,128)}), f32[16,1,16896]{2,1,0:T(1,128)}, u32[]{:S(2)}, u32[]{:S(2)}) %all-to-all-start) | async-done | bytes 1081376 | tf_op jit(solution)/shard_map/all_to_all | solution.py:11
  39.0 0.8 stack.3
  39.8 11.5 %all-to-all-start.4 = ((bf16[16,2048,4]{1,2,0:T(4,128)(2,1)}), bf16[16,2048,4]{1,2,0:T(4,128)(2,1)S(1)}, u32[]{:S(2)}, u32[]{:S(2)}) async-start(bf16[16,2048,4]{1,2,0:T(4,128)(2,1)} %stack.3), calls=%async_computation.4 | async-start | bytes 524288 | tf_op jit(solution)/shard_map/all_to_all | solution.py:82
  51.4 1.9 %reduce_sum.39 = f32[16896]{0:T(1024)S(1)} reduce(f32[16,1,16896]{2,1,0:T(1,128)} %all-to-all-done, f32[]{:T(128)} %constant.6.clone.1), dimensions={0,1}, to_apply=%region_3.0 | reduce | flops 253440 | bytes 1148932 | tf_op jit(solution)/shard_map/reduce_sum | solution.py:15
  53.3 1.2 copy.43
  54.5 1.2 copy.45
  55.7 1.2 copy.50
  56.8 0.0 copy-done.2
  56.8 7.7 %fusion = bf16[4,1408,128]{2,0,1:T(4,128)(2,1)} fusion(f32[4,1408,128]{2,1,0:T(8,128)S(1)} %copy-done.2, f32[4,1408]{0,1:T(8,128)} %copy.50), kind=kLoop, calls=%fused_computation.5 | loop fusion | flops 1441792 | bytes 4347904 | tf_op jit(solution)/shard_map/convert_element_type | solution.py:66
  64.6 0.0 copy-start.3
  64.6 0.0 all-to-all-done.4
  64.6 4.7 %all-to-all-start.2 = ((bf16[4,1408,128]{2,0,1:T(4,128)(2,1)}), bf16[4,1408,128]{2,0,1:T(4,128)(2,1)}, u32[]{:S(2)}, u32[]{:S(2)}) async-start(bf16[4,1408,128]{2,0,1:T(4,128)(2,1)} %fusion), calls=%async_computation.2 | async-start | bytes 2883584 | tf_op jit(solution)/shard_map/all_to_all | solution.py:69
  69.3 0.0 copy-done.3
  69.3 6.6 %divide_convert_fusion = (bf16[4,128,1408]{1,0,2:T(4,128)(2,1)S(1)}, bf16[4,128,1408]{1,0,2:T(4,128)(2,1)S(1)}) fusion(f32[4,128,1408]{1,0,2:T(4,128)} %copy.46, f32[4,1408]{0,1:T(8,128)} %copy.45, f32[4,128,1408]{1,0,2:T(4,128)S(1)} %copy-done.3, f32[4,1408]{0,1:T(8,128)} %copy.43), kind=kLoop, calls=%fused_computation.6 | loop fusion | flops 2883584 | bytes 8695808 | tf_op jit(solution)/shard_map/convert_element_type | solution.py:65
  75.8 2.6 %pad_maximum_fusion = bf16[8,128,1408]{1,0,2:T(8,128)(2,1)} fusion(bf16[4,128,1408]{1,0,2:T(4,128)(2,1)S(1)} %get-tuple-element.12, bf16[4,128,1408]{1,0,2:T(4,128)(2,1)S(1)} %get-tuple-element.13), kind=kLoop, calls=%fused_computation | loop fusion | flops 5767168 | bytes 5767168 | tf_op jit(solution)/shard_map/concatenate | solution.py:28
  78.5 15.3 %all-to-all-done.2 = bf16[4,1408,128]{2,0,1:T(4,128)(2,1)} async-done(((bf16[4,1408,128]{2,0,1:T(4,128)(2,1)}), bf16[4,1408,128]{2,0,1:T(4,128)(2,1)}, u32[]{:S(2)}, u32[]{:S(2)}) %all-to-all-start.2) | async-done | bytes 1441824 | tf_op jit(solution)/shard_map/all_to_all | solution.py:69
  93.8 3.7 %all-to-all-start.1 = ((bf16[8,128,1408]{1,0,2:T(8,128)(2,1)}), bf16[8,128,1408]{1,0,2:T(8,128)(2,1)S(1)}, u32[]{:S(2)}, u32[]{:S(2)}) async-start(bf16[8,128,1408]{1,0,2:T(8,128)(2,1)} %pad_maximum_fusion), calls=%async_computation.1 | async-start | bytes 5767168 | tf_op jit(solution)/shard_map/all_to_all | solution.py:30
  97.5 0.8 reshape.81
  98.3 0.6 constant_dynamic-slice_fusion.2
  98.9 0.7 constant_dynamic-slice_fusion
  99.6 3.0 %copy.52 = bf16[4,88,16,128]{3,2,1,0:T(8,128)(2,1)} copy(bf16[4,88,16,128]{3,0,1,2:T(4,128)(2,1)} %bitcast.4) | data formatting | bytes 2883584 | tf_op jit(solution)/shard_map/all_to_all | solution.py:69
  102.6 3.5 %all_to_all.41 = bf16[4,88,2048]{2,1,0:T(8,128)(2,1)} reshape(bf16[4,88,16,128]{3,2,1,0:T(8,128)(2,1)} %copy.52) | data formatting | bytes 2883584 | tf_op jit(solution)/shard_map/all_to_all | solution.py:69
  106.1 34.2 %all-to-all-done.1 = bf16[8,128,1408]{1,0,2:T(8,128)(2,1)S(1)} async-done(((bf16[8,128,1408]{1,0,2:T(8,128)(2,1)}), bf16[8,128,1408]{1,0,2:T(8,128)(2,1)S(1)}, u32[]{:S(2)}, u32[]{:S(2)}) %all-to-all-start.1) | async-done | bytes 2883616 | tf_op jit(solution)/shard_map/all_to_all | solution.py:30
  140.3 0.4 copy.47
  140.7 0.2 slice_bitcast_fusion
  140.9 1.5 %copy.64 = bf16[4,16,11,8,128]{4,3,1,2,0:T(8,128)(2,1)} copy(bf16[4,16,11,8,128]{4,3,2,1,0:T(8,128)(2,1)S(1)} %get-tuple-element.7) | data formatting | bytes 2883584 | tf_op jit(solution)/shard_map/slice | solution.py:35
  142.4 1.5 %copy.65 = bf16[4,16,11,8,128]{4,3,1,2,0:T(8,128)(2,1)} copy(bf16[4,16,11,8,128]{4,3,2,1,0:T(8,128)(2,1)S(1)} %get-tuple-element.8) | data formatting | bytes 2883584 | tf_op jit(solution)/shard_map/slice | solution.py:35
  (8 shorter events, 0.1 us)
Async XLA Ops:
  0.6 11.1 %copy-start.1 = (f32[4,128,1408]{2,1,0:T(8,128)S(1)}, f32[4,128,1408]{2,1,0:T(8,128)}, u32[]{:S(2)}) copy-start(f32[4,128,1408]{2,1,0:T(8,128)} %param.6) | copy-start | bytes 8650756
  2.1 14.0 %all-to-all-start.3 = ((bf16[16,128,4]{1,2,0:T(4,128)(2,1)}), bf16[16,128,4]{1,2,0:T(4,128)(2,1)S(1)}, u32[]{:S(2)}, u32[]{:S(2)}) async-start(bf16[16,128,4]{1,2,0:T(4,128)(2,1)} %broadcast_in_dim.5), calls=%async_computation.3 | async-start | bytes 32768 | tf_op jit(solution)/shard_map/all_to_all | solution.py:11
  12.0 11.1 %copy-start = (f32[4,128,1408]{2,1,0:T(8,128)S(1)}, f32[4,128,1408]{2,1,0:T(8,128)}, u32[]{:S(2)}) copy-start(f32[4,128,1408]{2,1,0:T(8,128)} %param.5) | copy-start | bytes 8650756
  17.7 21.4 %all-to-all-start = ((f32[16,1,16896]{2,1,0:T(1,128)}), f32[16,1,16896]{2,1,0:T(1,128)}, u32[]{:S(2)}, u32[]{:S(2)}) async-start(f32[16,1,16896]{2,1,0:T(1,128)} %broadcast_in_dim.4), calls=%async_computation | async-start | bytes 2162688 | tf_op jit(solution)/shard_map/all_to_all | solution.py:11
  30.5 26.4 %copy-start.2 = (f32[4,1408,128]{2,1,0:T(8,128)S(1)}, f32[4,1408,128]{2,1,0:T(8,128)}, u32[]{:S(2)}) copy-start(f32[4,1408,128]{2,1,0:T(8,128)} %param.7) | copy-start | bytes 8650756
  39.8 24.7 %all-to-all-start.4 = ((bf16[16,2048,4]{1,2,0:T(4,128)(2,1)}), bf16[16,2048,4]{1,2,0:T(4,128)(2,1)S(1)}, u32[]{:S(2)}, u32[]{:S(2)}) async-start(bf16[16,2048,4]{1,2,0:T(4,128)(2,1)} %stack.3), calls=%async_computation.4 | async-start | bytes 524288 | tf_op jit(solution)/shard_map/all_to_all | solution.py:82
  64.6 4.7 %copy-start.3 = (f32[4,128,1408]{1,0,2:T(4,128)S(1)}, f32[4,128,1408]{1,0,2:T(4,128)}, u32[]{:S(2)}) copy-start(f32[4,128,1408]{1,0,2:T(4,128)} %copy.44) | copy-start | bytes 8650756
  64.6 29.2 %all-to-all-start.2 = ((bf16[4,1408,128]{2,0,1:T(4,128)(2,1)}), bf16[4,1408,128]{2,0,1:T(4,128)(2,1)}, u32[]{:S(2)}, u32[]{:S(2)}) async-start(bf16[4,1408,128]{2,0,1:T(4,128)(2,1)} %fusion), calls=%async_computation.2 | async-start | bytes 2883584 | tf_op jit(solution)/shard_map/all_to_all | solution.py:69
  93.8 46.5 %all-to-all-start.1 = ((bf16[8,128,1408]{1,0,2:T(8,128)(2,1)}), bf16[8,128,1408]{1,0,2:T(8,128)(2,1)S(1)}, u32[]{:S(2)}, u32[]{:S(2)}) async-start(bf16[8,128,1408]{1,0,2:T(8,128)(2,1)} %pad_maximum_fusion), calls=%async_computation.1 | async-start | bytes 5767168 | tf_op jit(solution)/shard_map/all_to_all | solution.py:30
